TPU v7x, 32 devices: a 4x4x1 block of a 4x4x8 slice. The times are simulated.
32 devices in a mesh: data: 1 (over z), model: 4 (over y), beam: 8 (over x, core).
Axes of the slice: x: 4, y: 4, z: 1, core: 2. Of those that a mesh axis runs over, the one named last changes fastest.
The devices are a block of a 4x4x8 slice.
Arguments:
- x_embed: bfloat16 [32, 4096], P(('data', 'beam'))
- parent: int32 [1, 32], P('data')
- position: int32 [], replicated
- score: float32 [32], P(('data', 'beam'))
- k_cache: bfloat16 [1, 32, 512, 32, 128], P(None, ('data', 'beam'), None, 'model')
- v_cache: bfloat16 [1, 32, 512, 32, 128], P(None, ('data', 'beam'), None, 'model')
- gain_attn: bfloat16 [1, 4096], replicated
- w_query: bfloat16 [1, 4096, 4096], P(None, None, 'model')
- w_key: bfloat16 [1, 4096, 4096], P(None, None, 'model')
- w_value: bfloat16 [1, 4096, 4096], P(None, None, 'model')
- w_out: bfloat16 [1, 4096, 4096], P(None, 'model')
- gain_mlp: bfloat16 [1, 4096], replicated
- w_gate: bfloat16 [1, 4096, 11008], P(None, None, 'model')
- w_up: bfloat16 [1, 4096, 11008], P(None, None, 'model')
- w_down: bfloat16 [1, 11008, 4096], P(None, 'model')
- gain_final: bfloat16 [4096], replicated
- w_vocab: bfloat16 [4096, 32000], P(None, 'model')
Outputs:
- output 1: bfloat16 [1, 32, 512, 32, 128], P(None, ('data', 'beam'), None, 'model')
- output 2: bfloat16 [1, 32, 512, 32, 128], P(None, ('data', 'beam'), None, 'model')
- output 3: float32 [32, 32000], P(('data', 'beam'), 'model')
All inputs are finite; a program needn't handle non-finite values.
Results may differ from a plain program's by a relative error of at most 0.001.
Values are sent between devices in bfloat16 or wider.
A program may use at most 768 MiB of HBM per device.

v0:
```python
import functools
import types

import jax
import jax.numpy as jnp
from jax import lax
from jax.experimental import pallas as pl
from jax.experimental.pallas import tpu as pltpu
import numpy as np
from jax.sharding import PartitionSpec as P

NORM_EPS = 1e-6
ROPE_BASE = 10000.0
MESH = pl.DeviceIdType.MESH
CHUNKS = 8
TABLE = 24
ROUND_CHOICES = (3, 4)
W_BUFFERS = 4
SIDES = (0, 1)
LANES = 128
VMEM_LIMIT = 66 * 10**6


def plan_kernel(chips, chip_rows, parent_ref, table_ref, info_ref, hop_plus, hop_minus, onward, side):
    total = chips * chip_rows
    my_chip = lax.axis_index("beam") // 2
    row_bits, chip_mask, row_mask = chip_rows.bit_length() - 1, chips - 1, chip_rows - 1
    spare = 2 * TABLE + chip_rows

    near, far, back = [jnp.int32(0)] * 3
    parents = [parent_ref[0, b] for b in range(total)]
    for b, q in enumerate(parents):
        dist = ((b >> row_bits) - (q >> row_bits)) & chip_mask
        bit = jnp.left_shift(1, q)
        near |= jnp.where(dist == 1, bit, 0)
        far |= jnp.where(dist == 2, bit, 0)
        back |= jnp.where(dist == 3, bit, 0)

    def bit_of(mask, q):
        return jnp.right_shift(mask, q) & 1

    every = [(q, q >> row_bits, bit_of(near, q), bit_of(far, q), bit_of(back, q)) for q in range(total)]
    right = [(c + 1) & chip_mask for c in range(chips)]
    left = [(c - 1) & chip_mask for c in range(chips)]
    load_plus, load_minus, own_plus, own_minus, two_plus, two_minus = [[jnp.int32(0)] * chips for _ in range(6)]
    plus, minus = [], []
    for q, c, a, b, d in every:
        plus.append(b & a & (1 - d))
        minus.append(b & d & (1 - a))
        own_plus[c] += a
        own_minus[c] += d
        load_plus[right[c]] += plus[q]
        load_minus[left[c]] += minus[q]
    load_plus = [x + y for x, y in zip(load_plus, own_plus)]
    load_minus = [x + y for x, y in zip(load_minus, own_minus)]
    for q, c, a, b, d in every:
        flex = b & (1 - (a ^ d))
        cost_plus = jnp.maximum(load_plus[c] - a, load_plus[right[c]])
        cost_minus = jnp.maximum(load_minus[c] - d, load_minus[left[c]])
        go = jnp.where(cost_plus <= cost_minus, flex, 0)
        stay = flex - go
        for load, own, x, y in ((load_plus, own_plus, go, a), (load_minus, own_minus, stay, d)):
            load[c] += x & (1 - y)
            own[c] += x & (1 - y)
        load_plus[right[c]] += go
        load_minus[left[c]] += stay
        plus[q] += go
        minus[q] += stay
    first_plus, first_minus = [], []
    for q, c, *_ in every:
        first_plus.append(two_plus[c])
        first_minus.append(two_minus[c])
        two_plus[c] += plus[q]
        two_minus[c] += minus[q]
    rounds = jnp.int32(0)

    for at in range(spare):
        table_ref[at] = 0

    def write(cond, place, value):
        table_ref[jnp.where(cond, place, spare)] = value

    for q, c, a, b, d in every:
        a, d = a & (1 - plus[q]), d & (1 - minus[q])
        h_plus = jnp.where(a == 1, two_plus[c], first_plus[q])
        h_minus = jnp.where(d == 1, two_minus[c], first_minus[q])
        two_plus[c] += a
        two_minus[c] += d
        second = jnp.where(plus[q] == 1, jnp.maximum(own_plus[right[c]], 1) + h_plus, jnp.maximum(own_minus[left[c]], 1) + h_minus)
        uses_plus, uses_minus, uses_two = (a + plus[q]) == 1, (d + minus[q]) == 1, (plus[q] + minus[q]) == 1
        for use, h in ((uses_plus, h_plus), (uses_minus, h_minus), (uses_two, second)):
            rounds = jnp.maximum(rounds, jnp.where(use, h + 1, 0))
        hop_plus[q] = h_plus
        hop_minus[q] = h_minus
        onward[q] = second
        side[q] = plus[q]
        here = my_chip == c
        write(here & uses_plus, h_plus, q & row_mask)
        write(here & uses_minus, TABLE + h_minus, q & row_mask)
        write((my_chip == right[c]) & (plus[q] == 1), second, chip_rows + h_plus)
        write((my_chip == left[c]) & (minus[q] == 1), TABLE + second, chip_rows + h_minus)
    info_ref[0] = rounds
    for j in range(chip_rows):
        q = parent_ref[0, my_chip * chip_rows + j]
        dist = (my_chip - (q >> row_bits)) & chip_mask
        at_plus = chip_rows + 2 * jnp.where(dist == 1, hop_plus[q], onward[q])
        at_minus = chip_rows + 2 * jnp.where(dist == 3, hop_minus[q], onward[q]) + 1
        from_plus = (dist == 1) | ((dist == 2) & (side[q] == 1))
        table_ref[2 * TABLE + j] = jnp.where(dist == 0, q & row_mask, jnp.where(from_plus, at_plus, at_minus))


def make_plan(parent, chips, chip_rows):
    total = chips * chip_rows
    smem = pl.BlockSpec(memory_space=pltpu.SMEM)
    return pl.pallas_call(
        functools.partial(plan_kernel, chips, chip_rows),
        out_shape=(jax.ShapeDtypeStruct((2 * TABLE + chip_rows + 1,), jnp.int32), jax.ShapeDtypeStruct((1,), jnp.int32)),
        in_specs=[smem],
        out_specs=(smem, smem),
        scratch_shapes=[pltpu.SMEM((total,), jnp.int32)] * 4,
        name="plan",
    )(parent)


def loop(n, body):
    def step(i, carry):
        body(i)
        return carry

    lax.fori_loop(0, n, step, 0)


class Copies:
    def __init__(self, copies):
        self.copies = copies

    def start(self):
        for copy in self.copies:
            copy.start()

    def wait(self):
        for copy in self.copies:
            copy.wait()


def step_kernel(rounds, beams, models, rows, heads, slots, d_model, ff, vocab, names, *refs):
    r = types.SimpleNamespace(**dict(zip(names, refs)))
    table, pos_ref, parent_ref = r.table, r.pos, r.parent
    k_ref, v_ref, k_out, v_out = r.k, r.v, r.k_out, r.v_out
    f32, bf16 = jnp.float32, jnp.bfloat16
    nchunk = CHUNKS
    block = slots * heads // nchunk
    span = slots // nchunk
    chips = beams // 2
    pair = 2 * rows
    lanes = LANES
    me = lax.axis_index("beam")
    core = lax.rem(me, 2)
    chip = me // 2
    is_k, is_v = core == 0, core == 1
    all_half, all_heads = pl.ds(0, d_model // 2), pl.ds(0, heads * LANES)
    sibling = me + 1 - 2 * core
    right = lax.rem(me + 2, beams)
    left = lax.rem(me + beams - 2, beams)
    model = lax.axis_index("model")
    mine = pl.ds(core * rows, rows)
    theirs = pl.ds((1 - core) * rows, rows)
    lane_iota = lax.broadcasted_iota(jnp.int32, (1, lanes), 1)
    pool, recv, send, stage, other = r.pool, r.recv, r.send, r.stage, r.other
    half = d_model // 2

    def to(peer):
        return dict(device_id={"beam": peer}, device_id_type=MESH)

    def across(m, peer):
        return dict(device_id={"model": m, "beam": peer}, device_id_type=MESH)

    def part(ref, c):
        return ref.at[:, pl.ds(c * block, block), :]

    def load_own(ref, c):
        return pltpu.make_async_copy(part(ref, c), pool[c].at[mine], r.pool_sem.at[c])

    def load_other(ref, c):
        return pltpu.make_async_copy(part(ref, c), other[c], r.other_sem.at[c])

    def swap(ref, c):
        return pltpu.make_async_remote_copy(part(ref, c), pool[c].at[mine], r.swap_send.at[c], r.swap_recv.at[c], **to(sibling))

    def hop(n, d, c):
        return pltpu.make_async_remote_copy(
            send[c].at[2 * n + d], recv[c].at[2 * n + d], r.hop_send.at[n, d, c], r.hop_recv.at[n, d, c], **to(right if d == 0 else left))

    def store_own(ref, c):
        return pltpu.make_async_copy(stage[c].at[mine], part(ref, c), r.out_sem.at[c])

    def give(ref, c):
        return pltpu.make_async_remote_copy(stage[c].at[theirs], part(ref, c), r.give_send.at[c], r.give_recv.at[c], **to(sibling))

    w_count = len(r.wbuf)
    groups = []

    def group(blocks):
        groups.append(blocks)

    for ref in (r.w_query, r.w_key, r.w_value):
        width = heads * lanes // 2
        group([(ref, pl.ds(1024 * i, 1024), pl.ds(core * width, width), pl.ds(0, 1024), pl.ds(i * width, width)) for i in range(d_model // 1024)])
    group([(r.w_out, all_heads, pl.ds(core * half, half), all_heads, all_half)])
    ff_core = (ff + 127) // 256 * 128
    ff_full = ff_core // 256
    ff_last = ff_core - 256 * ff_full
    ff_skip = 2 * ff_core - ff
    for i in range(ff_full + 1):
        n = 256 if i < ff_full else ff_last
        first = core * (ff_core - (ff_skip if i == ff_full else 0)) + 256 * i
        first = pl.multiple_of(first, 8)
        group([(ref, pl.ds(first, n), pl.ds(j * half, half), pl.ds(512 * j + n * u, n), all_half) for u, ref in enumerate((r.w_gate, r.w_up)) for j in range(2)])
    down_rows = []
    for i in range(0, 2 * ff_core, 1024):
        n = min(1024, 2 * ff_core - i)
        down_rows.append((i, n))
        blocks = [(i, n, 0)]
        if i + n > 2 * ff_core - ff_last:
            blocks = [(i, n - ff_last, 0), (ff - ff_last, ff_last, n - ff_last)]
        group([(r.w_down, pl.ds(a, b), pl.ds(core * half, half), pl.ds(c, b), all_half) for a, b, c in blocks])
    voc_core = (vocab + 1023) // 1024 * 512
    voc_groups = voc_core // 512
    voc_skip = 2 * voc_core - vocab
    for i in range(voc_groups):
        first = core * (voc_core - (voc_skip if i == voc_groups - 1 else 0)) + 512 * i
        first = pl.multiple_of(first, 8)
        group([(r.w_vocab, pl.ds(first, 512), pl.ds(j * half, half), pl.ds(512 * j, 512), all_half) for j in range(2)])

    def group_copies(g):
        return [pltpu.make_async_copy(ref.at[a, b], r.wbuf[g % w_count].at[c, e], r.w_sem.at[g, i]) for i, (ref, a, b, c, e) in enumerate(groups[g])]

    def load(g):
        if g < len(groups):
            for copy in group_copies(g):
                copy.start()

    taken = [0]

    def with_group(use):
        g = taken[0]
        taken[0] += 1
        for copy in group_copies(g):
            copy.wait()
        use(r.wbuf[g % w_count])
        load(g + w_count)

    barrier = pltpu.get_barrier_semaphore()
    peers = [lax.rem(me + s, beams) for s in range(1, beams)]
    model_peers = [lax.rem(model + s, models) for s in range(1, models)]
    for peer in peers:
        pl.semaphore_signal(barrier, **to(peer))
    for m in model_peers:
        for peer in (me, sibling):
            pl.semaphore_signal(barrier, **across(m, peer))

    @pl.when(is_k)
    def _():
        for c in range(nchunk):
            load_own(k_ref, c).start()

    @pl.when(is_v)
    def _():
        for c in range(nchunk):
            load_own(v_ref, c).start()

    load(0)
    prow = jnp.zeros((1, lanes), jnp.int32)
    for b in range(beams * rows):
        prow = jnp.where(lax.rem(lane_iota, beams * rows) == b, parent_ref[0, b], prow)
    for j in range(rows):
        r.score_rows[j : j + 1, :] = jnp.full((1, lanes), r.score[j])
    angles = pos_ref[0].astype(f32) * r.freq[...]
    cos_part = jnp.cos(angles)
    sin_part = jnp.where(lane_iota < lanes // 2, -1.0, 1.0) * jnp.sin(angles)
    pl.semaphore_wait(barrier, beams - 1 + 2 * (models - 1))

    x_swap = pltpu.make_async_remote_copy(r.x, r.x_got, r.pair_send.at[0], r.pair_recv.at[0], **to(sibling))
    x_swap.start()

    @pl.when(is_k)
    def _():
        for c in range(nchunk):
            swap(v_ref, c).start()

    @pl.when(is_v)
    def _():
        for c in range(nchunk):
            swap(k_ref, c).start()

    for g in range(1, w_count):
        load(g)

    @pl.when(is_k)
    def _():
        for c in range(nchunk):
            load_other(v_ref, c).start()

    @pl.when(is_v)
    def _():
        for c in range(nchunk):
            load_other(k_ref, c).start()

    strip = min(block, 128)

    def build(n, c):
        for d in SIDES:
            code = table[d * TABLE + n]
            row = jnp.minimum(code, pair - 1)

            def body(i):
                at = pl.ds(pl.multiple_of(i * strip, strip), strip)
                x = pool[c][row, at, :]
                for e in range(n):
                    x = jnp.where(code == pair + e, recv[c][2 * e + d, at, :], x)
                send[c][2 * n + d, at, :] = x

            loop(block // strip, body)
        for d in SIDES:
            hop(n, d, c).start()

    waited = set()

    def have_own(c):
        if c not in waited:
            waited.add(c)
            load_own(k_ref, c).wait()

    def first_round(c):
        have_own(c)
        swap(k_ref, c).wait_recv()
        build(0, c)

    def later_round(n, c):
        for d in SIDES:
            hop(n - 1, d, c).wait_recv()
        build(n, c)

    def finish(c):
        for d in SIDES:
            hop(rounds - 1, d, c).wait_recv()
        position = pos_ref[0]

        def put_row(j):
            where = table[2 * TABLE + j]
            row = jnp.minimum(where, pair - 1)
            slot = jnp.clip(where - pair, 0, 2 * rounds - 1)
            new = jnp.concatenate([r.fresh[j]] * (strip // heads))

            def body(i):
                at = pl.ds(pl.multiple_of(i * strip, strip), strip)
                x = jnp.where(where < pair, pool[c][row, at, :], recv[c][slot, at, :])
                here = (lax.broadcasted_iota(jnp.int32, (strip, lanes), 0) + i * strip) // heads + c * span
                stage[c][j, at, :] = jnp.where(here == position, new, x.astype(f32)).astype(bf16)

            loop(block // strip, body)

        loop(pair, put_row)

        @pl.when(is_k)
        def _():
            give(k_out, c).start()
            store_own(k_out, c).start()

        @pl.when(is_v)
        def _():
            give(v_out, c).start()
            store_own(v_out, c).start()

    todo = [functools.partial(first_round, c) for c in range(nchunk)]
    todo += [functools.partial(later_round, n, c) for n in range(1, rounds) for c in range(nchunk)]
    todo += [functools.partial(finish, c) for c in range(nchunk)]

    def serve(n=1):
        for _ in range(n):
            if todo:
                todo.pop(0)()

    res = r.res

    def normed(gain_ref):
        x = res[...]
        inv = lax.rsqrt(jnp.mean(x * x, axis=-1, keepdims=True) + NORM_EPS)
        r.h[...] = (x * inv * gain_ref[...].astype(f32)).astype(bf16)

    def dot(a, b):
        return jnp.dot(a, b, preferred_element_type=f32)

    def dot_halves(w, n):
        def body(j, x):
            a = h[:, pl.ds(pl.multiple_of(j * half, lanes), half)]
            b = w[pl.ds(pl.multiple_of(j * 512, 512), n), :]
            return x + lax.dot_general(a, b, (((1,), (1,)), ((), ())), preferred_element_type=f32)

        return lax.fori_loop(0, 2, body, jnp.zeros((pair, n), f32))

    def dot_rows(a, first, w, n):
        def body(j, x):
            at = pl.multiple_of(j * (n // 2), lanes)
            return x + dot(a[:, pl.ds(first + at, n // 2)], w[pl.ds(at, n // 2), :])

        return lax.fori_loop(0, 2, body, jnp.zeros((pair, half), f32))

    def exchange_model(part_ref, got_ref, phase):
        if models == 1:
            return part_ref[...]
        copies = [
            pltpu.make_async_remote_copy(part_ref, got_ref.at[model], r.model_send.at[phase, s], r.model_recv.at[phase, s], **across(m, me))
            for s, m in enumerate(model_peers)]
        for copy in copies:
            copy.start()
        got_ref[model] = part_ref[...]
        for copy in copies:
            copy.wait()
        total = got_ref[0]
        for m in range(1, models):
            total = total + got_ref[m]
        return total

    serve()
    x_swap.wait()

    @pl.when(is_k)
    def _():
        res[0:rows, :] = r.x[...].astype(f32)
        res[rows:pair, :] = r.x_got[...].astype(f32)

    @pl.when(is_v)
    def _():
        res[0:rows, :] = r.x_got[...].astype(f32)
        res[rows:pair, :] = r.x[...].astype(f32)

    normed(r.gain_attn)
    h = r.h
    head_half = heads // 2
    width = head_half * lanes
    qkv = r.qkv
    for kind in range(3):
        def use(w, kind=kind):
            blocks = d_model // 1024
            each = min(2, blocks)

            def body(i, z):
                for e in range(each):
                    at = i * each + e
                    a = h[:, pl.ds(pl.multiple_of(at * 1024, 1024), 1024)]
                    z = z + dot(a, w[:, pl.ds(pl.multiple_of(at * width, lanes), width)])
                return z

            z = lax.fori_loop(0, blocks // each, body, jnp.zeros((pair, width), f32))
            for n in range(head_half):
                y = z[:, n * lanes : (n + 1) * lanes]
                if kind < 2:
                    y = y * cos_part + pltpu.roll(y, lanes // 2, 1) * sin_part
                qkv[kind, n] = y.astype(bf16)
        with_group(use)
    serve()

    qkv_all = r.qkv_all
    to_parents = Copies(
        [pltpu.make_async_remote_copy(qkv, qkv_all.at[me], r.beam_send.at[0, s], r.beam_recv.at[0, s], **to(p)) for s, p in enumerate(peers)]
        + [pltpu.make_async_remote_copy(r.score_rows, r.scores.at[me], r.beam_send.at[1, s], r.beam_recv.at[1, s], **to(p)) for s, p in enumerate(peers)])
    to_parents.start()
    qkv_all[me] = qkv[...]
    r.scores[me] = r.score_rows[...]
    serve(2)
    to_parents.wait()
    serve()

    cat = r.cat
    for kind in range(3):
        for n in range(heads):
            for x in range(chips):
                at = n * beams * rows + x * pair
                cat[kind, at : at + pair, :] = qkv_all[2 * x + n // head_half, kind, n % head_half].astype(f32)
    for j in range(pair):
        at = pl.ds(chip * pair + j, heads, stride=beams * rows)
        r.fresh[j] = jnp.where(is_k, cat[1, at, :], cat[2, at, :])

    query_t = cat[0].T.astype(bf16)
    new_k = cat[1].astype(bf16)
    total_cols = heads * beams * rows
    tiles = total_cols // lanes
    heads_tile = heads // tiles
    lane_head = lane_iota // (beams * rows)
    spread = r.spread
    logit = r.logit
    position = pos_ref[0]

    def own_rows(c, p, kind):
        a = pool[c][core * rows + p]
        b = other[c][p]
        return jnp.where(core == kind, a, b)

    def score_chunk(c):
        have_own(c)
        load_other(k_ref, c).wait()

        def body(p):
            full = dot(own_rows(c, p, 0), query_t)
            for t in range(tiles):
                spread[t][...] = full[:, t * lanes : (t + 1) * lanes]
            for t in range(tiles):
                here = prow == me * rows + p
                at = pl.ds(c * span, span)
                x = logit[t][at, :]
                for n in range(heads_tile):
                    got = spread[t][pl.ds(t * heads_tile + n, span, stride=heads), :]
                    x = jnp.where(here & (lane_head == n), got, x)
                logit[t][at, :] = x

        loop(rows, body)

    for t in range(tiles):
        logit[t][...] = jnp.zeros_like(logit[t])
    self_full = dot(new_k, query_t)
    scale = lanes ** -0.5
    for c in range(nchunk):
        score_chunk(c)
        serve(c % 4 == 3)
    slot_index = lax.broadcasted_iota(jnp.int32, (slots, lanes), 0)
    self_prob = []
    for t in range(tiles):
        diag = lax.broadcasted_iota(jnp.int32, (total_cols, lanes), 0) == lax.broadcasted_iota(jnp.int32, (total_cols, lanes), 1) + t * lanes
        self_row = jnp.sum(jnp.where(diag, self_full[:, t * lanes : (t + 1) * lanes], 0.0), axis=0, keepdims=True)
        x = jnp.where(slot_index == position, self_row, logit[t][...]) * scale
        x = jnp.where(slot_index <= position, x, -jnp.inf)
        e = jnp.exp(x - jnp.max(x, axis=0, keepdims=True))
        prob = e / jnp.sum(e, axis=0, keepdims=True)
        logit[t][...] = jnp.where(slot_index == position, 0.0, prob)
        self_prob.append(jnp.sum(jnp.where(slot_index == position, prob, 0.0), axis=0, keepdims=True))
    for t in range(tiles):
        spread[t][...] = jnp.zeros_like(spread[t])
    out_t = r.out_t
    out_t[...] = cat[2].T * jnp.concatenate(self_prob, axis=1).astype(bf16).astype(f32)

    def value_chunk(c):
        def body(p):
            for t in range(tiles):
                here = prow == me * rows + p
                x = logit[t][pl.ds(c * span, span), :]
                for n in range(heads_tile):
                    spread[t][pl.ds(t * heads_tile + n, span, stride=heads), :] = jnp.where(here & (lane_head == n), x, 0.0)
            prob = jnp.concatenate([spread[t][...].astype(bf16) for t in range(tiles)], axis=1)
            out_t[...] += lax.dot_general(own_rows(c, p, 1), prob, (((0,), (0,)), ((), ())), preferred_element_type=f32)

        loop(rows, body)

    for c in range(nchunk):
        value_chunk(c)
        serve(c % 3 == 1)
    local = jnp.concatenate([prow] * tiles, axis=1) // rows == me
    o_rows = jnp.where(local, out_t[...], 0.0).T
    o_send, o_got = r.o_send, r.o_got
    for x in range(chips):
        for n in range(heads):
            at = n * beams * rows + x * pair
            o_send[x, n] = o_rows[at : at + pair, :].astype(bf16)
    back = Copies([
        pltpu.make_async_remote_copy(o_send.at[lax.rem(me + s, beams) // 2], o_got.at[me], r.beam_send.at[2, s - 1], r.beam_recv.at[2, s - 1], **to(lax.rem(me + s, beams)))
        for s in range(1, beams)])
    back.start()
    o_got[me] = o_send[chip]
    serve(3)
    back.wait()
    for n in range(heads):
        x = o_got[0, n].astype(f32)
        for s in range(1, beams):
            x = x + o_got[s, n].astype(f32)
        r.o[:, n * lanes : (n + 1) * lanes] = x.astype(bf16)

    part_sum, model_got, res_half, res_got = r.part, r.model_got, r.res_half, r.res_got

    def add_to_residual(phase):
        total = exchange_model(part_sum, model_got.at[phase] if models > 1 else None, phase)
        col = pl.ds(pl.multiple_of(core * half, lanes), half)
        other_col = pl.ds(pl.multiple_of((1 - core) * half, lanes), half)
        fresh = res[:, col] + total
        res_half[phase] = fresh
        trade = pltpu.make_async_remote_copy(res_half.at[phase], res_got.at[phase], r.pair_send.at[1 + phase], r.pair_recv.at[1 + phase], **to(sibling))
        trade.start()
        res[:, col] = fresh
        trade.wait()
        res[:, other_col] = res_got[phase]

    def use_out(w):
        part_sum[0] = dot_rows(r.o, 0, w, heads * lanes)
    with_group(use_out)
    serve(2)
    part_sum_ref = part_sum
    part_sum = part_sum_ref.at[0]
    add_to_residual(0)
    serve(2)
    normed(r.gain_mlp)

    g_own, g_got, g_all = r.g_own, r.g_got, r.g_all
    for i in range(ff_full + 1):
        n = 256 if i < ff_full else ff_last

        def use(w, i=i, n=n):
            z = dot_halves(w, 2 * n)
            gate, up = z[:, :n], z[:, n:]
            y = jax.nn.silu(gate) * up
            if i == ff_full and ff_skip:
                y = jnp.where(is_v & (lax.broadcasted_iota(jnp.int32, (1, n), 1) < ff_skip), 0.0, y)
            g_own[:, 256 * i : 256 * i + n] = y.astype(bf16)
        with_group(use)
        serve(i == 2)
    g_trade = pltpu.make_async_remote_copy(g_own, g_got, r.pair_send.at[3], r.pair_recv.at[3], **to(sibling))
    g_trade.start()
    g_all[:, pl.ds(pl.multiple_of(core * ff_core, lanes), ff_core)] = g_own[...]
    serve()
    g_trade.wait()
    g_all[:, pl.ds(pl.multiple_of((1 - core) * ff_core, lanes), ff_core)] = g_got[...]
    part_sum = part_sum_ref.at[1]
    for at, n in down_rows:
        def use(w, at=at, n=n):
            x = dot_rows(g_all, at, w, n)
            part_sum[...] = x if at == 0 else part_sum[...] + x
        with_group(use)
    serve()
    add_to_residual(1)
    serve(2)
    normed(r.gain_final)

    word = r.word
    for i in range(voc_groups):
        def use(w, i=i):
            word[:, 512 * i : 512 * (i + 1)] = dot_halves(w, 512)
        with_group(use)
        serve(i > 2)
    word_send, word_got = r.word_send, r.word_got
    x = word[...]
    word_send[0] = x[0:rows]
    word_send[1] = x[rows:pair]
    word_trade = pltpu.make_async_remote_copy(word_send.at[1 - core], word_got, r.pair_send.at[4], r.pair_recv.at[4], **to(sibling))
    word_trade.start()
    col = lax.broadcasted_iota(jnp.int32, (1, voc_core), 1)
    twice = is_v & (col >= voc_core - 512) & (col < voc_core - 512 + voc_skip)
    x = jnp.where(twice, -jnp.inf, x)
    top = jnp.max(x, axis=-1, keepdims=True)
    mass = jnp.sum(jnp.exp(x - top), axis=-1, keepdims=True)
    stat, stats = r.stat, r.stats
    stat[0] = jnp.broadcast_to(top, (pair, lanes))
    stat[1] = jnp.broadcast_to(mass, (pair, lanes))
    mates = [(m, p) for m in [model] + model_peers for p in (me, sibling)][1:]
    told = Copies([
        pltpu.make_async_remote_copy(stat, stats.at[2 * model + core], r.stat_send.at[i], r.stat_recv.at[i], **across(m, p))
        for i, (m, p) in enumerate(mates)])
    told.start()
    stats[2 * model + core] = stat[...]
    told.wait()
    top = stats[0, 0]
    for i in range(1, 2 * models):
        top = jnp.maximum(top, stats[i, 0])
    mass = stats[0, 1] * jnp.exp(stats[0, 0] - top)
    for i in range(1, 2 * models):
        mass = mass + stats[i, 1] * jnp.exp(stats[i, 0] - top)
    r.stat[0] = top
    r.stat[1] = jnp.log(mass)
    word_trade.wait()
    own, got = word_send[core], word_got[...]
    low, high = jnp.where(is_k, own, got), jnp.where(is_k, got, own)
    last = voc_core - 512
    for j in range(rows):
        q = parent_ref[0, me * rows + j]
        base = r.scores[q // rows, pl.ds(lax.rem(q, rows), 1), :][:, 0:1]
        at = pl.ds(core * rows + j, 1)
        shift = stat[0, at, 0:1]
        log_mass = stat[1, at, 0:1]
        row = slice(j, j + 1)
        x = base + (high[row] - shift - log_mass)
        r.word_out[row, :voc_core] = base + (low[row] - shift - log_mass)
        r.word_out[row, voc_core : voc_core + last] = x[:, :last]
        r.word_out[row, voc_core + last :] = x[:, last + voc_skip :]

    serve(len(todo))
    for c in range(nchunk):
        swap(k_ref, c).wait_send()
        for n in range(rounds):
            for d in SIDES:
                hop(n, d, c).wait_send()
        store_own(k_out, c).wait()
        give(k_out, c).wait()


def run_step(rounds, beams, models, table, pos, parent, score, freq, x, k_rows, v_rows, gains, weights):
    rows, length, lanes = k_rows.shape
    weights_ = types.SimpleNamespace(**weights)
    d_model = x.shape[1]
    heads = weights_.w_query.shape[1] // lanes
    slots = length // heads
    ff = weights_.w_down.shape[0]
    vocab = weights_.w_vocab.shape[0]
    block = length // CHUNKS
    pair = 2 * rows
    half = d_model // 2
    chips = beams // 2
    cols = heads * beams * rows
    bf16, f32 = jnp.bfloat16, jnp.float32
    vmem, dma = pltpu.VMEM, pltpu.SemaphoreType.DMA
    smem, hbm, ram = (pl.BlockSpec(memory_space=s) for s in (pltpu.SMEM, pl.ANY, pltpu.VMEM))
    voc_core = (vocab + 1023) // 1024 * 512
    ff_core = (ff + 127) // 256 * 128
    n_groups = 4 + ff_core // 256 + 1 + -(-2 * ff_core // 1024) + voc_core // 512
    ins = dict(table=(table, smem), pos=(pos, smem), parent=(parent, smem), score=(score, smem), freq=(freq, ram),
               x=(x, ram), k=(k_rows, hbm), v=(v_rows, hbm))
    ins.update({name: (a, ram) for name, a in gains.items()})
    ins.update({name: (a, hbm) for name, a in weights.items()})
    outs = dict(k_out=(jax.ShapeDtypeStruct(k_rows.shape, bf16), hbm), v_out=(jax.ShapeDtypeStruct(k_rows.shape, bf16), hbm),
                word_out=(jax.ShapeDtypeStruct((rows, vocab), f32), ram))
    scratch = dict(
        pool=[vmem((pair, block, lanes), bf16)] * CHUNKS,
        recv=[vmem((2 * rounds, block, lanes), bf16)] * CHUNKS,
        send=[vmem((2 * rounds, block, lanes), bf16)] * CHUNKS,
        stage=[vmem((pair, block, lanes), bf16)] * CHUNKS,
        other=[vmem((rows, block, lanes), bf16)] * CHUNKS,
        wbuf=[vmem((1024, half), bf16)] * W_BUFFERS,
        spread=[vmem((block, lanes), f32)] * (cols // lanes),
        logit=[vmem((slots, lanes), f32)] * (cols // lanes),
        x_got=vmem(x.shape, bf16),
        res=vmem((pair, d_model), f32),
        h=vmem((pair, d_model), bf16),
        qkv=vmem((3, heads // 2, pair, lanes), bf16),
        qkv_all=vmem((beams, 3, heads // 2, pair, lanes), bf16),
        scores=vmem((beams, rows, lanes), f32),
        score_rows=vmem((rows, lanes), f32),
        cat=vmem((3, cols, lanes), f32),
        fresh=vmem((pair, heads, lanes), f32),
        out_t=vmem((lanes, cols), f32),
        o_send=vmem((chips, heads, pair, lanes), bf16),
        o_got=vmem((beams, heads, pair, lanes), bf16),
        o=vmem((pair, heads * lanes), bf16),
        part=vmem((2, pair, half), f32),
        model_got=vmem((2, models, pair, half), f32),
        res_half=vmem((2, pair, half), f32),
        res_got=vmem((2, pair, half), f32),
        g_own=vmem((pair, ff_core), bf16),
        g_got=vmem((pair, ff_core), bf16),
        g_all=vmem((pair, 2 * ff_core), bf16),
        word=vmem((pair, voc_core), f32),
        word_send=vmem((2, rows, voc_core), f32),
        word_got=vmem((rows, voc_core), f32),
        stat=vmem((2, pair, lanes), f32),
        stats=vmem((2 * models, 2, pair, lanes), f32),
        w_sem=dma((n_groups, 4)),
        pool_sem=dma((CHUNKS,)), other_sem=dma((CHUNKS,)), swap_send=dma((CHUNKS,)), swap_recv=dma((CHUNKS,)),
        hop_send=dma((rounds, 2, CHUNKS)), hop_recv=dma((rounds, 2, CHUNKS)),
        out_sem=dma((CHUNKS,)), give_send=dma((CHUNKS,)), give_recv=dma((CHUNKS,)),
        pair_send=dma((5,)), pair_recv=dma((5,)),
        beam_send=dma((3, beams)), beam_recv=dma((3, beams)),
        model_send=dma((2, models)), model_recv=dma((2, models)),
        stat_send=dma((2 * models,)), stat_recv=dma((2 * models,)),
    )
    flat, places = [], {}
    for name, s in scratch.items():
        many = isinstance(s, list)
        places[name] = (len(flat), len(s) if many else None)
        flat += s if many else [s]
    first = list(ins) + list(outs)

    def kernel(*refs):
        named = list(refs[: len(first)])
        rest = refs[len(first) :]
        for start, count in places.values():
            named.append(rest[start] if count is None else list(rest[start : start + count]))
        step_kernel(rounds, beams, models, rows, heads, slots, d_model, ff, vocab, first + list(places), *named)

    return pl.pallas_call(
        kernel,
        out_shape=tuple(s for s, _ in outs.values()),
        in_specs=[s for _, s in ins.values()],
        out_specs=tuple(s for _, s in outs.values()),
        scratch_shapes=flat,
        compiler_params=pltpu.CompilerParams(collective_id=rounds, has_side_effects=True, vmem_limit_bytes=VMEM_LIMIT),
        name=f"step{rounds}",
    )(*[a for a, _ in ins.values()])


def copy_kernel(pieces, a_ref, b_ref, a_out, b_out, buf, in_sem, out_sem):
    rows, length, _ = a_ref.shape
    per = rows // pieces
    jobs = [(src, dst, i) for i in range(pieces) for src, dst in ((a_ref, a_out), (b_ref, b_out))]

    def get(n):
        src, _, i = jobs[n]
        return pltpu.make_async_copy(src.at[pl.ds(i * per, per)], buf.at[n], in_sem.at[n])

    def put(n):
        _, dst, i = jobs[n]
        return pltpu.make_async_copy(buf.at[n], dst.at[pl.ds(i * per, per)], out_sem.at[n])

    for n in range(len(jobs)):
        get(n).start()
    for n in range(len(jobs)):
        get(n).wait()
        put(n).start()
    for n in range(len(jobs)):
        put(n).wait()


def settle(a, b):
    rows, length, lanes = a.shape
    hbm = pl.BlockSpec(memory_space=pl.ANY)
    out = jax.ShapeDtypeStruct(a.shape, a.dtype)
    return pl.pallas_call(
        functools.partial(copy_kernel, rows),
        out_shape=(out, out),
        in_specs=[hbm, hbm],
        out_specs=(hbm, hbm),
        scratch_shapes=[pltpu.VMEM((2 * rows, 1, length, lanes), a.dtype), pltpu.SemaphoreType.DMA((2 * rows,)), pltpu.SemaphoreType.DMA((2 * rows,))],
        name="settle",
    )(a, b)


def move_any(beams, heads, parent, position, k_rows, v_rows, k_new, v_new):
    rows, length, _ = k_rows.shape
    me = lax.axis_index("beam")
    mine = lax.dynamic_slice(parent.reshape(-1), (me * rows,), (rows,))
    local = lax.rem(mine, rows)
    ring = [(i, (i + 1) % beams) for i in range(beams)]

    def choose(source, here, chosen):
        hit = (mine // rows == source)[:, None, None]
        return jnp.where(hit, jnp.take(here, local, axis=0), chosen)

    def step(s, carry):
        k_here, v_here, k_sel, v_sel = carry
        source = lax.rem(me - s + beams, beams)
        k_sel, v_sel = choose(source, k_here, k_sel), choose(source, v_here, v_sel)
        return lax.ppermute(k_here, "beam", ring), lax.ppermute(v_here, "beam", ring), k_sel, v_sel

    carry = (lax.ppermute(k_rows, "beam", ring), lax.ppermute(v_rows, "beam", ring), choose(me, k_rows, k_new), choose(me, v_rows, v_new))
    carry = lax.fori_loop(1, beams, step, carry)
    written = (jnp.arange(length) // heads == position)[None, :, None]
    return jnp.where(written, k_new, carry[2]), jnp.where(written, v_new, carry[3])


def solution(mesh):
    beams = mesh.shape["beam"]
    models = mesh.shape["model"]
    cache_spec = P(None, ('data', 'beam'), None, 'model', None)
    col_spec = P(None, None, 'model')
    row_spec = P(None, 'model', None)
    in_specs = (P(('data', 'beam'), None), P('data', None), P(), P(('data', 'beam')), cache_spec, cache_spec,
                P(), col_spec, col_spec, col_spec, row_spec, P(), col_spec, col_spec, row_spec, P(), P(None, 'model'))
    out_specs = (cache_spec, cache_spec, P(('data', 'beam'), 'model'))

    def local_step(x_embed, parent, position, score, k_cache, v_cache, gain_attn, w_query, w_key, w_value, w_out, gain_mlp, w_gate, w_up, w_down, gain_final, w_vocab):
        rows = x_embed.shape[0]
        _, _, slots, heads, lanes = k_cache.shape
        table, info = make_plan(parent, beams // 2, 2 * rows)
        k_rows = k_cache.reshape(rows, slots * heads, lanes)
        v_rows = v_cache.reshape(rows, slots * heads, lanes)
        half_dim = lanes // 2
        freq = np.float32(ROPE_BASE) ** (-np.arange(half_dim, dtype=np.float32) / np.float32(half_dim))
        freq = jnp.asarray(np.concatenate([freq, freq])[None])
        pos = position.reshape(1)
        gains = dict(gain_attn=gain_attn, gain_mlp=gain_mlp, gain_final=gain_final.reshape(1, -1))
        weights = dict(w_query=w_query[0], w_key=w_key[0], w_value=w_value[0], w_out=w_out[0],
                       w_gate=w_gate[0].T, w_up=w_up[0].T, w_down=w_down[0], w_vocab=w_vocab.T)
        def step(rounds):
            return run_step(rounds, beams, models, table, pos, parent, score, freq, x_embed, k_rows, v_rows, gains, weights)

        def few(_):
            k_new, v_new, word = step(ROUND_CHOICES[0])
            return *settle(k_new, v_new), word

        def more(_):
            k_new, v_new, word = step(ROUND_CHOICES[1])
            enough = info[0] <= ROUND_CHOICES[1]
            k_new, v_new = lax.cond(enough, settle, lambda a, b: move_any(beams, heads, parent, position, k_rows, v_rows, a, b), k_new, v_new)
            return k_new, v_new, word

        k_new, v_new, candidates = lax.cond(info[0] <= ROUND_CHOICES[0], few, more, 0)
        shape = (1, rows, slots, heads, lanes)
        return k_new.reshape(shape), v_new.reshape(shape), candidates

    return jax.shard_map(local_step, mesh=mesh, in_specs=in_specs, out_specs=out_specs, check_vma=False)
```

profile of v0, /device:TPU:97, one launch (start us, length us, event | category | flops | bytes accessed | tf_op | source)
XLA Modules:
  0.0 121.6 jit_solution(14244651944524181706)
XLA Ops:
  0.6 2.7 %plan.1 = (s32[57]{0:T(128)S(1)}, s32[1]{0:T(128)}) custom-call(s32[1,32]{1,0:T(1,128)} %parent_ref.1), custom_call_target="tpu_custom_call" | custom-call | tf_op jit(solution)/shard_map/plan/pallas_call | solution.py:115
  3.3 0.7 reshape.143
  4.7 116.2 %conditional.2 = (bf16[4,4096,128]{2,1,0:T(8,128)(2,1)}, bf16[4,4096,128]{2,1,0:T(8,128)(2,1)}, f32[4,8000]{1,0:T(4,128)S(1)}) conditional(s32[]{:T(128)} %bitcast.6, (s32[1]{0:T(128)}, s32[57]{0:T(128)S(1)}, s32[1]{0:T(128)}, s32[1,32]{1,0:T(1,128)}, f32[4]{0:T(128)}, /*index=5*/f32[1,128]{1,0:T(1,128)}, bf16[4,4096]{1,0:T(4,128)(2,1)}, ...), branch_computations={%region_0.6_spmd, %region_5.7_spmd} | conditional | flops 21010650 | bytes 192956000 | solution.py:880
  4.9 109.6 %step3.1 = (bf16[4,4096,128]{2,1,0:T(8,128)(2,1)}, bf16[4,4096,128]{2,1,0:T(8,128)(2,1)}, f32[4,8000]{1,0:T(4,128)S(1)}) custom-call(s32[57]{0:T(128)S(1)} %get-tuple-element.370.refs_0_, s32[1]{0:T(128)} %get-tuple-element.371.refs_1_, s32[1,32]{1,0:T(1,128)} %get-tuple-element.372.refs_2_, f32[4]{0:T(128)} %get-tuple-element.373.refs_3_, ...), custom_call_target="tpu_custom_call" | custom-call | tf_op jit(solution)/shard_map/cond/branch_1_fun/step3/pallas_call | solution.py:774
  114.5 6.4 %settle.3 = (bf16[4,4096,128]{2,1,0:T(8,128)(2,1)}, bf16[4,4096,128]{2,1,0:T(8,128)(2,1)}) custom-call(bf16[4,4096,128]{2,1,0:T(8,128)(2,1)} %get-tuple-element.389.a_ref, bf16[4,4096,128]{2,1,0:T(8,128)(2,1)} %get-tuple-element.390.b_ref), custom_call_target="tpu_custom_call" | custom-call | tf_op jit(solution)/shard_map/cond/branch_1_fun/settle/pallas_call | solution.py:811
  120.9 0.7 copy.47
where the time goes:
time: 122 us
  Pallas kernels  119 us (98%)
  local copies, waits for them, and re-layouts  1.36 us (1%)
  between operations  1.3 us (1%)
    pallas_call x1, Pallas kernels, run_step(): pl.pallas_call(kernel, out_shape=tuple((s for s, _ in outs.values())), in...  110 us
    pallas_call x1, Pallas kernels, settle(): pl.pallas_call(functools.partial(copy_kernel, rows), out_shape=(out, out)...  6.42 us
    pallas_call x1, Pallas kernels, make_plan(): pl.pallas_call(functools.partial(plan_kernel, chips, chip_rows), out_shap...  2.69 us

commit v1 on v0

--- a/solution.py
+++ b/solution.py
@@ -15,7 +15,7 @@
 CHUNKS = 8
 TABLE = 24
 ROUND_CHOICES = (3, 4)
-W_BUFFERS = 4
+W_BUFFERS = 9
 SIDES = (0, 1)
 LANES = 128
 VMEM_LIMIT = 66 * 10**6
@@ -282,6 +282,9 @@
 
     x_swap = pltpu.make_async_remote_copy(r.x, r.x_got, r.pair_send.at[0], r.pair_recv.at[0], **to(sibling))
     x_swap.start()
+    tell_scores = Copies(
+        [pltpu.make_async_remote_copy(r.score_rows, r.scores.at[me], r.beam_send.at[1, s], r.beam_recv.at[1, s], **to(p)) for s, p in enumerate(peers)])
+    tell_scores.start()
 
     @pl.when(is_k)
     def _():
@@ -374,7 +377,6 @@
 
     todo = [functools.partial(first_round, c) for c in range(nchunk)]
     todo += [functools.partial(later_round, n, c) for n in range(1, rounds) for c in range(nchunk)]
-    todo += [functools.partial(finish, c) for c in range(nchunk)]
 
     def serve(n=1):
         for _ in range(n):
@@ -415,6 +417,7 @@
         for copy in copies:
             copy.start()
         got_ref[model] = part_ref[...]
+        serve(2)
         for copy in copies:
             copy.wait()
         total = got_ref[0]
@@ -459,18 +462,15 @@
                     y = y * cos_part + pltpu.roll(y, lanes // 2, 1) * sin_part
                 qkv[kind, n] = y.astype(bf16)
         with_group(use)
-    serve()
 
     qkv_all = r.qkv_all
     to_parents = Copies(
         [pltpu.make_async_remote_copy(qkv, qkv_all.at[me], r.beam_send.at[0, s], r.beam_recv.at[0, s], **to(p)) for s, p in enumerate(peers)]
-        + [pltpu.make_async_remote_copy(r.score_rows, r.scores.at[me], r.beam_send.at[1, s], r.beam_recv.at[1, s], **to(p)) for s, p in enumerate(peers)])
+        )
     to_parents.start()
     qkv_all[me] = qkv[...]
-    r.scores[me] = r.score_rows[...]
     serve(2)
     to_parents.wait()
-    serve()
 
     cat = r.cat
     for kind in range(3):
@@ -522,7 +522,7 @@
     scale = lanes ** -0.5
     for c in range(nchunk):
         score_chunk(c)
-        serve(c % 4 == 3)
+        serve(c == nchunk // 2)
     slot_index = lax.broadcasted_iota(jnp.int32, (slots, lanes), 0)
     self_prob = []
     for t in range(tiles):
@@ -553,7 +553,7 @@
 
     for c in range(nchunk):
         value_chunk(c)
-        serve(c % 3 == 1)
+        serve(c % 4 == 0)
     local = jnp.concatenate([prow] * tiles, axis=1) // rows == me
     o_rows = jnp.where(local, out_t[...], 0.0).T
     o_send, o_got = r.o_send, r.o_got
@@ -595,7 +595,6 @@
     part_sum_ref = part_sum
     part_sum = part_sum_ref.at[0]
     add_to_residual(0)
-    serve(2)
     normed(r.gain_mlp)
 
     g_own, g_got, g_all = r.g_own, r.g_got, r.g_all
@@ -610,11 +609,11 @@
                 y = jnp.where(is_v & (lax.broadcasted_iota(jnp.int32, (1, n), 1) < ff_skip), 0.0, y)
             g_own[:, 256 * i : 256 * i + n] = y.astype(bf16)
         with_group(use)
-        serve(i == 2)
+        serve(i % 2)
     g_trade = pltpu.make_async_remote_copy(g_own, g_got, r.pair_send.at[3], r.pair_recv.at[3], **to(sibling))
     g_trade.start()
+    serve()
     g_all[:, pl.ds(pl.multiple_of(core * ff_core, lanes), ff_core)] = g_own[...]
-    serve()
     g_trade.wait()
     g_all[:, pl.ds(pl.multiple_of((1 - core) * ff_core, lanes), ff_core)] = g_got[...]
     part_sum = part_sum_ref.at[1]
@@ -623,9 +622,8 @@
             x = dot_rows(g_all, at, w, n)
             part_sum[...] = x if at == 0 else part_sum[...] + x
         with_group(use)
-    serve()
+    serve(2)
     add_to_residual(1)
-    serve(2)
     normed(r.gain_final)
 
     word = r.word
@@ -633,7 +631,7 @@
         def use(w, i=i):
             word[:, 512 * i : 512 * (i + 1)] = dot_halves(w, 512)
         with_group(use)
-        serve(i > 2)
+        serve(i % 2)
     word_send, word_got = r.word_send, r.word_got
     x = word[...]
     word_send[0] = x[0:rows]
@@ -654,6 +652,9 @@
         for i, (m, p) in enumerate(mates)])
     told.start()
     stats[2 * model + core] = stat[...]
+    serve(len(todo))
+    for c in range(nchunk // 2):
+        finish(c)
     told.wait()
     top = stats[0, 0]
     for i in range(1, 2 * models):
@@ -664,6 +665,8 @@
     r.stat[0] = top
     r.stat[1] = jnp.log(mass)
     word_trade.wait()
+    tell_scores.wait()
+    r.scores[me] = r.score_rows[...]
     own, got = word_send[core], word_got[...]
     low, high = jnp.where(is_k, own, got), jnp.where(is_k, got, own)
     last = voc_core - 512
@@ -679,7 +682,8 @@
         r.word_out[row, voc_core : voc_core + last] = x[:, :last]
         r.word_out[row, voc_core + last :] = x[:, last + voc_skip :]
 
-    serve(len(todo))
+    for c in range(nchunk // 2, nchunk):
+        finish(c)
     for c in range(nchunk):
         swap(k_ref, c).wait_send()
         for n in range(rounds):
@@ -720,7 +724,7 @@
         send=[vmem((2 * rounds, block, lanes), bf16)] * CHUNKS,
         stage=[vmem((pair, block, lanes), bf16)] * CHUNKS,
         other=[vmem((rows, block, lanes), bf16)] * CHUNKS,
-        wbuf=[vmem((1024, half), bf16)] * W_BUFFERS,
+        wbuf=[vmem((1024, half), bf16)] * (W_BUFFERS - rounds),
         spread=[vmem((block, lanes), f32)] * (cols // lanes),
         logit=[vmem((slots, lanes), f32)] * (cols // lanes),
         x_got=vmem(x.shape, bf16),

time: 122 us -> 111 us (0.910)
  Pallas kernels: 119 us -> 108 us
    pallas_call x1, Pallas kernels: 110 us -> 98.9 us  [run_step(): pl.pallas_call(kernel, out_shape=tuple((s for s, _ in outs.values())), in...]
where the time goes in v1:
time: 111 us
  Pallas kernels  108 us (97%)
  local copies, waits for them, and re-layouts  1.36 us (1%)
  between operations  1.3 us (1%)
    pallas_call x1, Pallas kernels, run_step(): pl.pallas_call(kernel, out_shape=tuple((s for s, _ in outs.values())), in...  98.9 us
    pallas_call x1, Pallas kernels, settle(): pl.pallas_call(functools.partial(copy_kernel, rows), out_shape=(out, out)...  6.42 us
    pallas_call x1, Pallas kernels, make_plan(): pl.pallas_call(functools.partial(plan_kernel, chips, chip_rows), out_shap...  2.69 us

profile of v1, /device:TPU:97, one launch (start us, length us, event | category | flops | bytes accessed | tf_op | source)
XLA Modules:
  0.0 110.9 jit_solution(12913100217035715409)
XLA Ops:
  0.6 2.7 %plan.1 = (s32[57]{0:T(128)S(1)}, s32[1]{0:T(128)}) custom-call(s32[1,32]{1,0:T(1,128)} %parent_ref.1), custom_call_target="tpu_custom_call" | custom-call | tf_op jit(solution)/shard_map/plan/pallas_call | solution.py:115
  3.3 0.7 reshape.143
  4.7 105.6 %conditional.2 = (bf16[4,4096,128]{2,1,0:T(8,128)(2,1)}, bf16[4,4096,128]{2,1,0:T(8,128)(2,1)}, f32[4,8000]{1,0:T(4,128)S(1)}) conditional(s32[]{:T(128)} %bitcast.6, (s32[1]{0:T(128)}, s32[57]{0:T(128)S(1)}, s32[1]{0:T(128)}, s32[1,32]{1,0:T(1,128)}, f32[4]{0:T(128)}, /*index=5*/f32[1,128]{1,0:T(1,128)}, bf16[4,4096]{1,0:T(4,128)(2,1)}, ...), branch_computations={%region_0.6_spmd, %region_5.7_spmd} | conditional | flops 21010650 | bytes 192956000 | solution.py:884
  4.9 98.9 %step3.1 = (bf16[4,4096,128]{2,1,0:T(8,128)(2,1)}, bf16[4,4096,128]{2,1,0:T(8,128)(2,1)}, f32[4,8000]{1,0:T(4,128)S(1)}) custom-call(s32[57]{0:T(128)S(1)} %get-tuple-element.370.refs_0_, s32[1]{0:T(128)} %get-tuple-element.371.refs_1_, s32[1,32]{1,0:T(1,128)} %get-tuple-element.372.refs_2_, f32[4]{0:T(128)} %get-tuple-element.373.refs_3_, ...), custom_call_target="tpu_custom_call" | custom-call | tf_op jit(solution)/shard_map/cond/branch_1_fun/step3/pallas_call | solution.py:778
  103.8 6.4 %settle.3 = (bf16[4,4096,128]{2,1,0:T(8,128)(2,1)}, bf16[4,4096,128]{2,1,0:T(8,128)(2,1)}) custom-call(bf16[4,4096,128]{2,1,0:T(8,128)(2,1)} %get-tuple-element.389.a_ref, bf16[4,4096,128]{2,1,0:T(8,128)(2,1)} %get-tuple-element.390.b_ref), custom_call_target="tpu_custom_call" | custom-call | tf_op jit(solution)/shard_map/cond/branch_1_fun/settle/pallas_call | solution.py:815
  110.3 0.7 copy.47

commit v2 on v1

--- a/solution.py
+++ b/solution.py
@@ -16,6 +16,7 @@
 TABLE = 24
 ROUND_CHOICES = (3, 4)
 W_BUFFERS = 9
+SETTLE_PIECES = 4
 SIDES = (0, 1)
 LANES = 128
 VMEM_LIMIT = 66 * 10**6
@@ -462,6 +463,7 @@
                     y = y * cos_part + pltpu.roll(y, lanes // 2, 1) * sin_part
                 qkv[kind, n] = y.astype(bf16)
         with_group(use)
+        serve(kind == 1)
 
     qkv_all = r.qkv_all
     to_parents = Copies(
@@ -522,7 +524,7 @@
     scale = lanes ** -0.5
     for c in range(nchunk):
         score_chunk(c)
-        serve(c == nchunk // 2)
+        serve(c % 4 == 1)
     slot_index = lax.broadcasted_iota(jnp.int32, (slots, lanes), 0)
     self_prob = []
     for t in range(tiles):
@@ -788,16 +790,16 @@
 
 def copy_kernel(pieces, a_ref, b_ref, a_out, b_out, buf, in_sem, out_sem):
     rows, length, _ = a_ref.shape
-    per = rows // pieces
-    jobs = [(src, dst, i) for i in range(pieces) for src, dst in ((a_ref, a_out), (b_ref, b_out))]
+    per = length // pieces
+    jobs = [(src, dst, i, e) for i in range(rows) for e in range(pieces) for src, dst in ((a_ref, a_out), (b_ref, b_out))]
 
     def get(n):
-        src, _, i = jobs[n]
-        return pltpu.make_async_copy(src.at[pl.ds(i * per, per)], buf.at[n], in_sem.at[n])
+        src, _, i, e = jobs[n]
+        return pltpu.make_async_copy(src.at[i, pl.ds(e * per, per)], buf.at[n], in_sem.at[n])
 
     def put(n):
-        _, dst, i = jobs[n]
-        return pltpu.make_async_copy(buf.at[n], dst.at[pl.ds(i * per, per)], out_sem.at[n])
+        _, dst, i, e = jobs[n]
+        return pltpu.make_async_copy(buf.at[n], dst.at[i, pl.ds(e * per, per)], out_sem.at[n])
 
     for n in range(len(jobs)):
         get(n).start()
@@ -812,12 +814,13 @@
     rows, length, lanes = a.shape
     hbm = pl.BlockSpec(memory_space=pl.ANY)
     out = jax.ShapeDtypeStruct(a.shape, a.dtype)
+    jobs = 2 * rows * SETTLE_PIECES
     return pl.pallas_call(
-        functools.partial(copy_kernel, rows),
+        functools.partial(copy_kernel, SETTLE_PIECES),
         out_shape=(out, out),
         in_specs=[hbm, hbm],
         out_specs=(hbm, hbm),
-        scratch_shapes=[pltpu.VMEM((2 * rows, 1, length, lanes), a.dtype), pltpu.SemaphoreType.DMA((2 * rows,)), pltpu.SemaphoreType.DMA((2 * rows,))],
+        scratch_shapes=[pltpu.VMEM((jobs, length // SETTLE_PIECES, lanes), a.dtype), pltpu.SemaphoreType.DMA((jobs,)), pltpu.SemaphoreType.DMA((jobs,))],
         name="settle",
     )(a, b)
 

time: 111 us -> 113 us (1.018)
  Pallas kernels: 108 us -> 110 us
    pallas_call x1, Pallas kernels: 98.9 us -> 100 us  [run_step(): pl.pallas_call(kernel, out_shape=tuple((s for s, _ in outs.values())), in...]
where the time goes in v2:
time: 113 us
  Pallas kernels  110 us (97%)
  local copies, waits for them, and re-layouts  1.36 us (1%)
  between operations  1.3 us (1%)
    pallas_call x1, Pallas kernels, run_step(): pl.pallas_call(kernel, out_shape=tuple((s for s, _ in outs.values())), in...  100 us
    pallas_call x1, Pallas kernels, settle(): pl.pallas_call(functools.partial(copy_kernel, SETTLE_PIECES), out_shape=(...  7.01 us
    pallas_call x1, Pallas kernels, make_plan(): pl.pallas_call(functools.partial(plan_kernel, chips, chip_rows), out_shap...  2.69 us

profile of v2, /device:TPU:97, one launch (start us, length us, event | category | flops | bytes accessed | tf_op | source)
XLA Modules:
  0.0 113.0 jit_solution(16245924224213752141)
XLA Ops:
  0.6 2.7 %plan.1 = (s32[57]{0:T(128)S(1)}, s32[1]{0:T(128)}) custom-call(s32[1,32]{1,0:T(1,128)} %parent_ref.1), custom_call_target="tpu_custom_call" | custom-call | tf_op jit(solution)/shard_map/plan/pallas_call | solution.py:116
  3.3 0.7 reshape.143
  4.7 107.7 %conditional.2 = (bf16[4,4096,128]{2,1,0:T(8,128)(2,1)}, bf16[4,4096,128]{2,1,0:T(8,128)(2,1)}, f32[4,8000]{1,0:T(4,128)S(1)}) conditional(s32[]{:T(128)} %bitcast.6, (s32[1]{0:T(128)}, s32[57]{0:T(128)S(1)}, s32[1]{0:T(128)}, s32[1,32]{1,0:T(1,128)}, f32[4]{0:T(128)}, /*index=5*/f32[1,128]{1,0:T(1,128)}, bf16[4,4096]{1,0:T(4,128)(2,1)}, ...), branch_computations={%region_0.6_spmd, %region_5.7_spmd} | conditional | flops 21010650 | bytes 192956000 | solution.py:887
  4.9 100.4 %step3.1 = (bf16[4,4096,128]{2,1,0:T(8,128)(2,1)}, bf16[4,4096,128]{2,1,0:T(8,128)(2,1)}, f32[4,8000]{1,0:T(4,128)S(1)}) custom-call(s32[57]{0:T(128)S(1)} %get-tuple-element.370.refs_0_, s32[1]{0:T(128)} %get-tuple-element.371.refs_1_, s32[1,32]{1,0:T(1,128)} %get-tuple-element.372.refs_2_, f32[4]{0:T(128)} %get-tuple-element.373.refs_3_, ...), custom_call_target="tpu_custom_call" | custom-call | tf_op jit(solution)/shard_map/cond/branch_1_fun/step3/pallas_call | solution.py:780
  105.3 7.0 %settle.3 = (bf16[4,4096,128]{2,1,0:T(8,128)(2,1)}, bf16[4,4096,128]{2,1,0:T(8,128)(2,1)}) custom-call(bf16[4,4096,128]{2,1,0:T(8,128)(2,1)} %get-tuple-element.389.a_ref, bf16[4,4096,128]{2,1,0:T(8,128)(2,1)} %get-tuple-element.390.b_ref), custom_call_target="tpu_custom_call" | custom-call | tf_op jit(solution)/shard_map/cond/branch_1_fun/settle/pallas_call | solution.py:818
  112.4 0.7 copy.47

commit v3 on v2

--- a/solution.py
+++ b/solution.py
@@ -15,8 +15,8 @@
 CHUNKS = 8
 TABLE = 24
 ROUND_CHOICES = (3, 4)
-W_BUFFERS = 9
-SETTLE_PIECES = 4
+W_BUFFERS = 8
+SETTLE_PIECES = 1
 SIDES = (0, 1)
 LANES = 128
 VMEM_LIMIT = 66 * 10**6
@@ -271,9 +271,6 @@
             load_own(v_ref, c).start()
 
     load(0)
-    prow = jnp.zeros((1, lanes), jnp.int32)
-    for b in range(beams * rows):
-        prow = jnp.where(lax.rem(lane_iota, beams * rows) == b, parent_ref[0, b], prow)
     for j in range(rows):
         r.score_rows[j : j + 1, :] = jnp.full((1, lanes), r.score[j])
     angles = pos_ref[0].astype(f32) * r.freq[...]
@@ -484,80 +481,64 @@
         at = pl.ds(chip * pair + j, heads, stride=beams * rows)
         r.fresh[j] = jnp.where(is_k, cat[1, at, :], cat[2, at, :])
 
-    query_t = cat[0].T.astype(bf16)
-    new_k = cat[1].astype(bf16)
-    total_cols = heads * beams * rows
-    tiles = total_cols // lanes
-    heads_tile = heads // tiles
-    lane_head = lane_iota // (beams * rows)
-    spread = r.spread
+    query = cat[0].astype(bf16)
+    group = beams * rows
+    total_rows = heads * group
+    pcol = jnp.zeros((group, lanes), jnp.int32)
+    for b in range(group):
+        pcol = jnp.where(lax.broadcasted_iota(jnp.int32, (group, lanes), 0) == b, parent_ref[0, b], pcol)
+    pcol = jnp.concatenate([pcol] * heads)[:, 0:1]
     logit = r.logit
     position = pos_ref[0]
 
     def own_rows(c, p, kind):
-        a = pool[c][core * rows + p]
-        b = other[c][p]
-        return jnp.where(core == kind, a, b)
+        return jnp.where(core == kind, pool[c][core * rows + p], other[c][p])
 
     def score_chunk(c):
         have_own(c)
         load_other(k_ref, c).wait()
+        at = pl.ds(c * block, block)
 
         def body(p):
-            full = dot(own_rows(c, p, 0), query_t)
-            for t in range(tiles):
-                spread[t][...] = full[:, t * lanes : (t + 1) * lanes]
-            for t in range(tiles):
-                here = prow == me * rows + p
-                at = pl.ds(c * span, span)
-                x = logit[t][at, :]
-                for n in range(heads_tile):
-                    got = spread[t][pl.ds(t * heads_tile + n, span, stride=heads), :]
-                    x = jnp.where(here & (lane_head == n), got, x)
-                logit[t][at, :] = x
+            full = lax.dot_general(query, own_rows(c, p, 0), (((1,), (1,)), ((), ())), preferred_element_type=f32)
+            logit[:, at] = jnp.where(pcol == me * rows + p, full, logit[:, at])
 
         loop(rows, body)
 
-    for t in range(tiles):
-        logit[t][...] = jnp.zeros_like(logit[t])
-    self_full = dot(new_k, query_t)
-    scale = lanes ** -0.5
     for c in range(nchunk):
+        logit[:, c * block : (c + 1) * block] = jnp.zeros((total_rows, block), f32)
         score_chunk(c)
         serve(c % 4 == 1)
-    slot_index = lax.broadcasted_iota(jnp.int32, (slots, lanes), 0)
-    self_prob = []
-    for t in range(tiles):
-        diag = lax.broadcasted_iota(jnp.int32, (total_cols, lanes), 0) == lax.broadcasted_iota(jnp.int32, (total_cols, lanes), 1) + t * lanes
-        self_row = jnp.sum(jnp.where(diag, self_full[:, t * lanes : (t + 1) * lanes], 0.0), axis=0, keepdims=True)
-        x = jnp.where(slot_index == position, self_row, logit[t][...]) * scale
-        x = jnp.where(slot_index <= position, x, -jnp.inf)
-        e = jnp.exp(x - jnp.max(x, axis=0, keepdims=True))
-        prob = e / jnp.sum(e, axis=0, keepdims=True)
-        logit[t][...] = jnp.where(slot_index == position, 0.0, prob)
-        self_prob.append(jnp.sum(jnp.where(slot_index == position, prob, 0.0), axis=0, keepdims=True))
-    for t in range(tiles):
-        spread[t][...] = jnp.zeros_like(spread[t])
-    out_t = r.out_t
-    out_t[...] = cat[2].T * jnp.concatenate(self_prob, axis=1).astype(bf16).astype(f32)
+    scale = lanes ** -0.5
+    r.self_logit[...] = jnp.broadcast_to(jnp.sum(cat[0] * cat[1], axis=-1, keepdims=True), (total_rows, lanes))
+    col = lax.broadcasted_iota(jnp.int32, (1, slots * heads), 1)
+    slot_of, head_of = col // heads, lax.rem(col, heads)
+
+    def soften(n):
+        at = pl.ds(pl.multiple_of(n * group, group), group)
+        x = jnp.where(slot_of == position, r.self_logit[at, 0:1], logit[at, :]) * scale
+        x = jnp.where((slot_of <= position) & (head_of == n), x, -jnp.inf)
+        e = jnp.exp(x - jnp.max(x, axis=-1, keepdims=True))
+        prob = e / jnp.sum(e, axis=-1, keepdims=True)
+        logit[at, :] = jnp.where(slot_of == position, 0.0, prob)
+        own = jnp.sum(jnp.where(slot_of == position, prob, 0.0), axis=-1, keepdims=True)
+        r.out[at, :] = cat[2, at, :] * own.astype(bf16).astype(f32)
+
+    loop(heads, soften)
 
     def value_chunk(c):
+        at = pl.ds(c * block, block)
+
         def body(p):
-            for t in range(tiles):
-                here = prow == me * rows + p
-                x = logit[t][pl.ds(c * span, span), :]
-                for n in range(heads_tile):
-                    spread[t][pl.ds(t * heads_tile + n, span, stride=heads), :] = jnp.where(here & (lane_head == n), x, 0.0)
-            prob = jnp.concatenate([spread[t][...].astype(bf16) for t in range(tiles)], axis=1)
-            out_t[...] += lax.dot_general(own_rows(c, p, 1), prob, (((0,), (0,)), ((), ())), preferred_element_type=f32)
+            prob = jnp.where(pcol == me * rows + p, logit[:, at], 0.0).astype(bf16)
+            r.out[...] += dot(prob, own_rows(c, p, 1))
 
         loop(rows, body)
 
     for c in range(nchunk):
         value_chunk(c)
         serve(c % 4 == 0)
-    local = jnp.concatenate([prow] * tiles, axis=1) // rows == me
-    o_rows = jnp.where(local, out_t[...], 0.0).T
+    o_rows = jnp.where(pcol // rows == me, r.out[...], 0.0)
     o_send, o_got = r.o_send, r.o_got
     for x in range(chips):
         for n in range(heads):
@@ -727,8 +708,8 @@
         stage=[vmem((pair, block, lanes), bf16)] * CHUNKS,
         other=[vmem((rows, block, lanes), bf16)] * CHUNKS,
         wbuf=[vmem((1024, half), bf16)] * (W_BUFFERS - rounds),
-        spread=[vmem((block, lanes), f32)] * (cols // lanes),
-        logit=[vmem((slots, lanes), f32)] * (cols // lanes),
+        logit=vmem((cols, length), f32),
+        self_logit=vmem((cols, lanes), f32),
         x_got=vmem(x.shape, bf16),
         res=vmem((pair, d_model), f32),
         h=vmem((pair, d_model), bf16),
@@ -738,7 +719,7 @@
         score_rows=vmem((rows, lanes), f32),
         cat=vmem((3, cols, lanes), f32),
         fresh=vmem((pair, heads, lanes), f32),
-        out_t=vmem((lanes, cols), f32),
+        out=vmem((cols, lanes), f32),
         o_send=vmem((chips, heads, pair, lanes), bf16),
         o_got=vmem((beams, heads, pair, lanes), bf16),
         o=vmem((pair, heads * lanes), bf16),

time: 113 us -> 117 us (1.035)
  Pallas kernels: 110 us -> 114 us
    pallas_call x1, Pallas kernels: 100 us -> 105 us  [run_step(): pl.pallas_call(kernel, out_shape=tuple((s for s, _ in outs.values())), in...]
where the time goes in v3:
time: 117 us
  Pallas kernels  114 us (97%)
  local copies, waits for them, and re-layouts  1.36 us (1%)
  between operations  1.3 us (1%)
    pallas_call x1, Pallas kernels, run_step(): pl.pallas_call(kernel, out_shape=tuple((s for s, _ in outs.values())), in...  105 us
    pallas_call x1, Pallas kernels, settle(): pl.pallas_call(functools.partial(copy_kernel, SETTLE_PIECES), out_shape=(...  6.42 us
    pallas_call x1, Pallas kernels, make_plan(): pl.pallas_call(functools.partial(plan_kernel, chips, chip_rows), out_shap...  2.69 us

profile of v3, /device:TPU:97, one launch (start us, length us, event | category | flops | bytes accessed | tf_op | source)
XLA Modules:
  0.0 117.0 jit_solution(11846011704745353974)
XLA Ops:
  0.6 2.7 %plan.1 = (s32[57]{0:T(128)S(1)}, s32[1]{0:T(128)}) custom-call(s32[1,32]{1,0:T(1,128)} %parent_ref.1), custom_call_target="tpu_custom_call" | custom-call | tf_op jit(solution)/shard_map/plan/pallas_call | solution.py:116
  3.3 0.7 reshape.143
  4.7 111.7 %conditional.2 = (bf16[4,4096,128]{2,1,0:T(8,128)(2,1)}, bf16[4,4096,128]{2,1,0:T(8,128)(2,1)}, f32[4,8000]{1,0:T(4,128)S(1)}) conditional(s32[]{:T(128)} %bitcast.6, (s32[1]{0:T(128)}, s32[57]{0:T(128)S(1)}, s32[1]{0:T(128)}, s32[1,32]{1,0:T(1,128)}, f32[4]{0:T(128)}, /*index=5*/f32[1,128]{1,0:T(1,128)}, bf16[4,4096]{1,0:T(4,128)(2,1)}, ...), branch_computations={%region_0.6_spmd, %region_5.7_spmd} | conditional | flops 21010650 | bytes 192956000 | solution.py:868
  4.9 105.0 %step3.1 = (bf16[4,4096,128]{2,1,0:T(8,128)(2,1)}, bf16[4,4096,128]{2,1,0:T(8,128)(2,1)}, f32[4,8000]{1,0:T(4,128)S(1)}) custom-call(s32[57]{0:T(128)S(1)} %get-tuple-element.370.refs_0_, s32[1]{0:T(128)} %get-tuple-element.371.refs_1_, s32[1,32]{1,0:T(1,128)} %get-tuple-element.372.refs_2_, f32[4]{0:T(128)} %get-tuple-element.373.refs_3_, ...), custom_call_target="tpu_custom_call" | custom-call | tf_op jit(solution)/shard_map/cond/branch_1_fun/step3/pallas_call | solution.py:761
  109.9 6.4 %settle.3 = (bf16[4,4096,128]{2,1,0:T(8,128)(2,1)}, bf16[4,4096,128]{2,1,0:T(8,128)(2,1)}) custom-call(bf16[4,4096,128]{2,1,0:T(8,128)(2,1)} %get-tuple-element.389.a_ref, bf16[4,4096,128]{2,1,0:T(8,128)(2,1)} %get-tuple-element.390.b_ref), custom_call_target="tpu_custom_call" | custom-call | tf_op jit(solution)/shard_map/cond/branch_1_fun/settle/pallas_call | solution.py:799
  116.4 0.7 copy.47
